TPU v7x, 32 devices: a whole 2x2x4 slice. The times are simulated.
32 devices in a mesh: seq: 8 (over z, x), kvh: 4 (over y, core).
Axes of the slice: x: 2, y: 2, z: 4, core: 2. Of those that a mesh axis runs over, the one named last changes fastest.
Arguments:
- queries: bfloat16 [1024, 28, 128], P('seq', 'kvh'), may hold values from -80 to 80
- new_keys: bfloat16 [1024, 4, 128], P('seq', 'kvh'), may hold values from -8 to 8
- cache_keys: bfloat16 [512, 4, 128], P('seq', 'kvh'), may hold values from -1.1953125 to 1.1953125
- window_start: int32 [8], replicated, may hold values from 0 to 512, as said below
- owner_slot: int32 [8], replicated, may hold values from 0 to 511, as said below
Outputs:
- relevance: bfloat16 [1024, 28, 512], P('seq', 'kvh')
- rep_bank: bfloat16 [512, 4, 128], P('seq', 'kvh')
Inputs may be any that keep to these rules, and one draw needn't show every extreme that they name: `window_start`: each window lies inside the new tokens; some window begins at the first new token and some ends at the last. `owner_slot`: the slots are distinct; the first and the last memory block are always among them.
All inputs are finite; a program needn't handle non-finite values.
Results may differ from a plain program's by a relative error of at most 0.0018.
Values may be sent and summed in bfloat16 or wider, within the bound.
A program may use at most 64 MiB of HBM per device.

v0:
```python
import math

import jax
import jax.numpy as jnp
from jax import lax
from jax.sharding import PartitionSpec as P

BLK = 128
WIN = 512


def row_scores(query_rows, key_rows):
    return lax.dot_general(
        query_rows, key_rows, (((1,), (1,)), ((), ())), preferred_element_type=jnp.float32
    )


def per_device(queries, new_keys, cache_keys, window_start, owner_slot):
    tok_count, group_size, head_dim = queries.shape
    score_scale = 1.0 / math.sqrt(head_dim)
    query_rows = queries.reshape(tok_count * group_size, head_dim)
    device_index = lax.axis_index("seq")
    keys_all = lax.all_gather(new_keys, "seq", axis=0, tiled=True)
    key_flat = keys_all[:, 0, :]
    total_tokens = key_flat.shape[0]
    block_count = total_tokens // BLK
    group_blocks = math.gcd(block_count, 8)
    position = device_index * tok_count + jnp.arange(tok_count, dtype=jnp.int32)
    row_position = jnp.repeat(position, group_size)
    inside = (row_position[:, None] >= window_start[None, :]) & (
        row_position[:, None] < window_start[None, :] + WIN
    )
    inside = inside.astype(jnp.float32)
    key_groups = key_flat.reshape(block_count // group_blocks, group_blocks * BLK, head_dim)
    inside_groups = inside.reshape(
        query_rows.shape[0], block_count // group_blocks, group_blocks
    ).transpose(1, 0, 2)

    def group_sums(members):
        key_part, mask_part = members
        scores = row_scores(query_rows, key_part) * score_scale
        scores = scores.reshape(query_rows.shape[0], group_blocks, BLK)
        softmax_weights = jax.nn.softmax(scores, axis=-1)
        return jnp.einsum("rgk,rg->gk", softmax_weights, mask_part)

    colsum = lax.map(group_sums, (key_groups, inside_groups)).reshape(block_count, BLK)
    colsum = lax.psum(colsum, "seq")
    weights = colsum / (group_size * WIN)
    representative = jnp.einsum(
        "nr,nrz->nz",
        weights,
        key_flat.reshape(block_count, BLK, head_dim).astype(jnp.float32),
        precision=lax.Precision.HIGHEST,
    ).astype(jnp.bfloat16)
    rep_float = representative.astype(jnp.float32)
    local_blocks = cache_keys.shape[0]
    slot_ids = device_index * local_blocks + jnp.arange(local_blocks, dtype=jnp.int32)
    matches = (owner_slot[:, None] == slot_ids[None, :]).astype(jnp.float32)
    placed = jnp.dot(matches.T, rep_float, precision=lax.Precision.HIGHEST)
    slot_taken = jnp.sum(matches, axis=0) > 0.5
    new_shard = jnp.where(slot_taken[:, None], placed.astype(jnp.bfloat16), cache_keys[:, 0, :])
    totals = (
        row_scores(query_rows, lax.all_gather(new_shard, "seq", axis=0, tiled=True)) * score_scale
    )
    relevance = totals.astype(jnp.bfloat16).reshape(tok_count, group_size, totals.shape[1])
    return (relevance, new_shard[:, None, :])


def solution(mesh):
    return jax.shard_map(
        per_device,
        mesh=mesh,
        in_specs=(P("seq", "kvh", None), P("seq", "kvh", None), P("seq", "kvh", None), P(), P()),
        out_specs=(P("seq", "kvh", None), P("seq", "kvh", None)),
        check_vma=False,
    )
```

profile of v0, /device:TPU:0, one launch (start us, length us, event | category | flops | bytes accessed | tf_op | source)
XLA Modules:
  0.0 238.6 jit_solution(1154057495097289812)
XLA Ops:
  0.6 1.1 copy.14
  1.7 0.1 reshape.33
  1.8 32.8 %all_gather.6 = bf16[1024,1,128]{2,0,1:T(8,128)(2,1)S(1)} all-gather(bf16[128,1,128]{2,0,1:T(8,128)(2,1)} %param.6), channel_id=1, replica_groups=mesh['seq'=8,'kvh'=4] {'seq'}, dimensions={0}, use_global_device_ids=true | all-gather | bytes 294912 | tf_op jit(solution)/shard_map/all_gather | solution.py:23
  34.6 0.6 multiply_bitcast_fusion
  35.2 0.9 copy.22
  36.1 145.2 %fusion.12 = (f32[896,8]{1,0:T(8,128)S(1)}, f32[896,8,128]{2,1,0:T(8,128)S(1)}) fusion(f32[896,8,128]{2,1,0:T(8,128)S(1)} %bitcast.27), kind=kOutput, calls=%fused_computation.24 | output fusion | flops 1835135 | bytes 7368704 | tf_op jit(solution)/shard_map/while/body/eval_jaxpr/sub | solution.py:43
  181.3 0.0 copy-start.1
  181.3 0.0 copy-start.3
  181.3 0.0 copy-start.2
  181.4 1.2 broadcast_divide_fusion
  182.6 0.1 broadcast_in_dim.28
  182.7 0.2 ge.15
  182.9 0.1 and_bitcast_fusion
  183.0 0.5 fusion.1
  183.5 21.4 %psum.7 = f32[8,128]{1,0:T(8,128)S(1)} all-reduce(f32[8,128]{1,0:T(8,128)S(1)} %bitcast.32), channel_id=1, replica_groups=mesh['seq'=8,'kvh'=4] {'seq'}, use_global_device_ids=true, to_apply=%region_3.4 | all-reduce | flops 1024 | bytes 8192 | tf_op jit(solution)/shard_map/psum | solution.py:47
  204.9 0.3 fusion.13
  205.2 0.1 fusion.8
  205.3 0.3 fusion.4
  205.6 0.0 copy-start
  205.6 30.5 %all_gather.7 = bf16[512,128]{1,0:T(8,128)(2,1)S(1)} all-gather(bf16[64,128]{1,0:T(8,128)(2,1)S(1)} %fusion.4), channel_id=1, replica_groups=mesh['seq'=8,'kvh'=4] {'seq'}, dimensions={0}, use_global_device_ids=true | all-gather | bytes 147456 | tf_op jit(solution)/shard_map/all_gather | solution.py:63
  236.1 0.4 fusion.3
  236.5 0.5 copy.15
  237.0 0.3 reshape.35
  237.3 1.2 copy.16
  (9 shorter events, 0.0 us)
Async XLA Ops:
  181.3 1.6 copy-start.1
  181.3 23.9 %copy-start.3 = (s32[8]{0:T(128)S(1)}, s32[8]{0:T(128)}, u32[]{:S(2)}) copy-start(s32[8]{0:T(128)} %param.9) | copy-start | bytes 100
  181.3 24.0 %copy-start.2 = (bf16[64,1,128]{2,0,1:T(8,128)(2,1)S(1)}, bf16[64,1,128]{2,0,1:T(8,128)(2,1)}, u32[]{:S(2)}) copy-start(bf16[64,1,128]{2,0,1:T(8,128)(2,1)} %param.7) | copy-start | bytes 49156
  205.6 33.0 %copy-start = (bf16[64,128]{1,0:T(8,128)(2,1)}, bf16[64,128]{1,0:T(8,128)(2,1)S(1)}, u32[]{:S(2)}) copy-start(bf16[64,128]{1,0:T(8,128)(2,1)S(1)} %fusion.4) | copy-start | bytes 49156
where the time goes:
time: 239 us
  other arithmetic  147 us (62%)
  blocking collectives  84.7 us (35%)
  local copies, waits for them, and re-layouts  4.46 us (2%)
    sub x1, other arithmetic, group_sums(): softmax_weights = jax.nn.softmax(scores, axis=-1)  145 us
    all_gather x1, blocking collectives, per_device(): keys_all = lax.all_gather(new_keys, 'seq', axis=0, tiled=True)  32.8 us
    all_gather x1, blocking collectives, per_device(): lax.all_gather(new_shard, 'seq', axis=0, tiled=True)  30.5 us
    psum x1, blocking collectives, per_device(): colsum = lax.psum(colsum, 'seq')  21.4 us

commit v1 on v0

v1 whole, which is shorter than its diff:
```python
import functools
import math

import jax
import jax.numpy as jnp
from jax import lax
from jax.experimental import pallas as pl
from jax.experimental.pallas import tpu as pltpu
from jax.sharding import PartitionSpec as P

BLK = 128
WIN = 512
LOG2E = 1.4426950408889634
NT = (((1,), (1,)), ((), ()))


def each(count, body):
    if count <= 8:
        for i in range(count):
            body(i)
    else:
        lax.fori_loop(0, count, lambda i, c: (body(i), c)[1], 0)


def refresh_kernel(
    n, start_ref, slot_ref, q_hbm, k_hbm, c_hbm, rel_ref, bank_ref,
    q_v, q_t, keys, cache, mine, parts, bank,
    load_sem, ks_sem, kr_sem, cs_sem, cr_sem, ps_sem, pr_sem,
):
    group, toks, dim = q_v.shape
    ktoks = keys.shape[1]
    local = cache.shape[1]
    slots = n * local
    per = ktoks // BLK
    blocks = n * per
    rows = group * toks
    scale = 1.0 / math.sqrt(dim)
    me = lax.axis_index("seq")

    load_k = pltpu.make_async_copy(k_hbm, keys.at[me], load_sem.at[0])
    load_q = pltpu.make_async_copy(q_hbm, q_v, load_sem.at[1])
    load_c = pltpu.make_async_copy(c_hbm, cache.at[me], load_sem.at[2])
    load_k.start()
    load_q.start()
    load_c.start()

    barrier = pltpu.get_barrier_semaphore()

    def greet(i):
        peer = lax.rem(me + 1 + i, n)
        pl.semaphore_signal(
            barrier, inc=1, device_id={"seq": peer}, device_id_type=pl.DeviceIdType.MESH
        )

    each(n - 1, greet)

    def link(src, dst, s_sem, r_sem, peer):
        return pltpu.make_async_remote_copy(
            src_ref=src, dst_ref=dst, send_sem=s_sem, recv_sem=r_sem,
            device_id={"seq": peer}, device_id_type=pl.DeviceIdType.MESH,
        )

    def key_copy(slot, peer):
        return link(keys.at[slot], keys.at[slot], ks_sem.at[peer], kr_sem.at[slot], peer)

    def cache_copy(slot, peer):
        return link(cache.at[slot], cache.at[slot], cs_sem.at[peer], cr_sem.at[slot], peer)

    def part_copy(slot, peer, src):
        return link(src, parts.at[slot], ps_sem.at[peer], pr_sem.at[slot], peer)

    load_k.wait()
    pl.semaphore_wait(barrier, n - 1)
    each(n - 1, lambda i: key_copy(me, lax.rem(me + 1 + i, n)).start())
    load_c.wait()
    each(n - 1, lambda i: cache_copy(me, lax.rem(me + 1 + i, n)).start())

    load_q.wait()
    for j in range(group):
        q_t[:, j * toks:(j + 1) * toks] = q_v[j].T

    position = me * toks + lax.broadcasted_iota(jnp.int32, (1, toks), 1)

    def partial(owner):
        for p in range(per):
            index = owner * per + p
            kb = keys[owner, p * BLK:(p + 1) * BLK, :]
            begin = start_ref[index]
            mask = jnp.where((position >= begin) & (position < begin + WIN), 1.0, 0.0)
            s = jnp.dot(kb, q_t[...], preferred_element_type=jnp.float32)
            top = jnp.max(s, axis=0, keepdims=True)
            e = jnp.exp2((s - top) * (scale * LOG2E))
            total = jnp.sum(e, axis=0, keepdims=True)
            acc = None
            for j in range(group):
                cols = slice(j * toks, (j + 1) * toks)
                term = e[:, cols] * (mask / total[:, cols])
                acc = term if acc is None else acc + term
            weight = jnp.sum(acc, axis=1, keepdims=True)
            rep = jnp.sum(weight * kb.astype(jnp.float32), axis=0, keepdims=True)
            mine[pl.ds(index, 1), :] = rep

    partial(me)

    def arrive(i):
        owner = lax.rem(me + n - 1 - i, n)
        key_copy(owner, owner).wait_recv()
        partial(owner)

    each(n - 1, arrive)
    each(n - 1, lambda i: part_copy(me, lax.rem(me + 1 + i, n), mine).start())

    each(n - 1, lambda i: cache_copy(lax.rem(me + n - 1 - i, n), me).wait_recv())
    hits = jnp.where(
        lax.broadcasted_iota(jnp.int32, (slots, blocks), 0) == slot_ref[...], 1.0, 0.0
    )
    taken = jnp.max(hits, axis=1, keepdims=True)
    hits = hits.astype(jnp.bfloat16)
    old = cache[...].reshape(slots, dim)

    each(n - 1, lambda i: part_copy(lax.rem(me + n - 1 - i, n), me, mine).wait_recv())
    parts[me] = mine[...]
    if n <= 8:
        rep_sum = parts[0]
        for d in range(1, n):
            rep_sum = rep_sum + parts[d]
    else:
        rep_sum = lax.fori_loop(1, n, lambda d, c: c + parts[d], parts[0])
    rep = (rep_sum * (1.0 / (group * WIN))).astype(jnp.bfloat16)
    placed = jnp.dot(hits, rep, preferred_element_type=jnp.float32)
    bank[...] = jnp.where(taken > 0.5, placed, old.astype(jnp.float32)).astype(jnp.bfloat16)
    bank_ref[...] = bank[pl.ds(pl.multiple_of(me * local, local), local), :]

    def relate(j):
        r = lax.dot_general(q_v[j], bank[...], NT, preferred_element_type=jnp.float32)
        rel_ref[j] = (r * scale).astype(jnp.bfloat16)

    each(group, relate)

    def drain(i):
        peer = lax.rem(me + 1 + i, n)
        key_copy(me, peer).wait_send()
        cache_copy(me, peer).wait_send()
        part_copy(me, peer, mine).wait_send()

    each(n - 1, drain)


def per_device(n, queries, new_keys, cache_keys, window_start, owner_slot):
    toks, group, dim = queries.shape
    ktoks, local = new_keys.shape[0], cache_keys.shape[0]
    blocks = window_start.shape[0]
    slots = n * local
    any_spec = pl.BlockSpec(memory_space=pl.ANY)
    vmem_spec = pl.BlockSpec(memory_space=pltpu.VMEM)
    bf16 = jnp.bfloat16
    rel, bank = pl.pallas_call(
        functools.partial(refresh_kernel, n),
        out_shape=(
            pltpu.VMEM((group, toks, slots), bf16),
            pltpu.VMEM((local, dim), bf16),
        ),
        in_specs=[
            pl.BlockSpec(memory_space=pltpu.SMEM), vmem_spec, any_spec, any_spec, any_spec,
        ],
        out_specs=(vmem_spec, vmem_spec),
        scratch_shapes=[
            pltpu.VMEM((group, toks, dim), bf16),
            pltpu.VMEM((dim, group * toks), bf16),
            pltpu.VMEM((n, ktoks, dim), bf16),
            pltpu.VMEM((n, local, dim), bf16),
            pltpu.VMEM((blocks, dim), jnp.float32),
            pltpu.VMEM((n, blocks, dim), jnp.float32),
            pltpu.VMEM((slots, dim), bf16),
            pltpu.SemaphoreType.DMA((3,)),
        ] + [pltpu.SemaphoreType.DMA((n,))] * 6,
        compiler_params=pltpu.CompilerParams(
            collective_id=0, has_side_effects=True, vmem_limit_bytes=40 * 1024 * 1024
        ),
        name="refresh",
    )(
        window_start,
        owner_slot.reshape(1, blocks),
        jnp.transpose(queries, (1, 0, 2)),
        new_keys.reshape(ktoks, dim),
        cache_keys.reshape(local, dim),
    )
    return jnp.transpose(rel, (1, 0, 2)), bank[:, None, :]


def solution(mesh):
    spec = P("seq", "kvh", None)
    return jax.shard_map(
        functools.partial(per_device, mesh.shape["seq"]),
        mesh=mesh,
        in_specs=(spec, spec, spec, P(), P()),
        out_specs=(spec, spec),
        check_vma=False,
    )
```

time: 239 us -> 28.5 us (0.12)
  other arithmetic: 147 us -> 0 us
  blocking collectives: 84.7 us -> 0 us
  Pallas kernels: 0 us -> 22.9 us
    sub x1 -> x0, other arithmetic: 145 us -> none  [group_sums(): softmax_weights = jax.nn.softmax(scores, axis=-1)]
    all_gather x2 -> x0, blocking collectives: 63.3 us -> none  [the longest x1 32.8 us: per_device(): keys_all = lax.all_gather(new_keys, 'seq', axis=0, tiled=True)]
    pallas_call x0 -> x1, Pallas kernels: none -> 22.9 us  [per_device(): pl.pallas_call(functools.partial(refresh_kernel, n), out_shape=(pltpu.VME...]
    psum x1 -> x0, blocking collectives: 21.4 us -> none  [per_device(): colsum = lax.psum(colsum, 'seq')]
where the time goes in v1:
time: 28.5 us; the launch traced here: 28.2 us
  Pallas kernels  22.9 us (80%)
  local copies, waits for them, and re-layouts  4.6 us (16%)
  between operations  0.66 us (2%)
    pallas_call x1, Pallas kernels, per_device(): pl.pallas_call(functools.partial(refresh_kernel, n), out_shape=(pltpu.VME...  22.9 us
    unnamed x12, local copies, waits for them, and re-layouts  4.6 us

profile of v1, /device:TPU:0, one launch (start us, length us, event | category | flops | bytes accessed | tf_op | source)
XLA Modules:
  0.0 28.2 jit_solution(15622717736815749543)
XLA Ops:
  0.6 0.0 copy-start.3
  0.6 0.0 copy-start.4
  0.7 0.6 %copy-done.3 = s32[8]{0:T(128)S(1)} copy-done((s32[8]{0:T(128)S(1)}, s32[8]{0:T(128)}, u32[]{:S(2)}) %copy-start.3) | copy-done | bytes 56
  1.3 0.0 copy-done.4
  1.3 0.0 copy-start
  1.3 0.9 %copy-done = bf16[128,7,128]{2,0,1:T(8,128)(2,1)S(1)} copy-done((bf16[128,7,128]{2,0,1:T(8,128)(2,1)S(1)}, bf16[128,7,128]{2,0,1:T(8,128)(2,1)}, u32[]{:S(2)}) %copy-start) | copy-done | bytes 229400
  2.2 0.0 copy-start.1
  2.2 0.8 %copy-done.1 = bf16[128,1,128]{2,0,1:T(8,128)(2,1)S(1)} copy-done((bf16[128,1,128]{2,0,1:T(8,128)(2,1)S(1)}, bf16[128,1,128]{2,0,1:T(8,128)(2,1)}, u32[]{:S(2)}) %copy-start.1) | copy-done | bytes 32792
  3.0 0.0 copy-start.2
  3.0 0.7 %copy-done.2 = bf16[64,1,128]{2,0,1:T(8,128)(2,1)S(1)} copy-done((bf16[64,1,128]{2,0,1:T(8,128)(2,1)S(1)}, bf16[64,1,128]{2,0,1:T(8,128)(2,1)}, u32[]{:S(2)}) %copy-start.2) | copy-done | bytes 16408
  3.7 22.9 %refresh.1 = (bf16[7,128,512]{2,1,0:T(8,128)(2,1)S(1)}, bf16[64,128]{1,0:T(8,128)(2,1)S(1)}) custom-call(s32[8]{0:T(128)S(1)} %copy-done.3, s32[1,8]{1,0:T(1,128)S(1)} %bitcast.11, bf16[7,128,128]{2,1,0:T(8,128)(2,1)S(1)} %bitcast.8, bf16[128,128]{1,0:T(8,128)(2,1)S(1)} %bitcast.9, bf16[64,128]{1,0:T(8,128)(2,1)S(1)} %bitcast.10), custom_call_target="tpu_custom_call" | custom-call | tf_op jit(solution)/shard_map/refresh/pallas_call | solution.py:157
  26.7 0.9 %copy.9 = bf16[128,7,512]{2,0,1:T(8,128)(2,1)} copy(bf16[128,7,512]{2,0,1:T(8,128)(2,1)S(1)} %bitcast.6) | data formatting | bytes 1835008
  27.6 0.6 %copy.10 = bf16[64,1,128]{2,0,1:T(8,128)(2,1)} copy(bf16[64,1,128]{2,0,1:T(8,128)(2,1)S(1)} %bitcast.7) | data formatting | bytes 32768
Async XLA Ops:
  0.6 0.7 %copy-start.3 = (s32[8]{0:T(128)S(1)}, s32[8]{0:T(128)}, u32[]{:S(2)}) copy-start(s32[8]{0:T(128)} %start_ref.1) | copy-start | bytes 100
  0.6 0.7 %copy-start.4 = (s32[8]{0:T(128)S(1)}, s32[8]{0:T(128)}, u32[]{:S(2)}) copy-start(s32[8]{0:T(128)} %param.9) | copy-start | bytes 100
  1.3 0.9 %copy-start = (bf16[128,7,128]{2,0,1:T(8,128)(2,1)S(1)}, bf16[128,7,128]{2,0,1:T(8,128)(2,1)}, u32[]{:S(2)}) copy-start(bf16[128,7,128]{2,0,1:T(8,128)(2,1)} %param.5) | copy-start | bytes 688132
  2.2 0.8 %copy-start.1 = (bf16[128,1,128]{2,0,1:T(8,128)(2,1)S(1)}, bf16[128,1,128]{2,0,1:T(8,128)(2,1)}, u32[]{:S(2)}) copy-start(bf16[128,1,128]{2,0,1:T(8,128)(2,1)} %param.6) | copy-start | bytes 98308
  3.0 0.7 %copy-start.2 = (bf16[64,1,128]{2,0,1:T(8,128)(2,1)S(1)}, bf16[64,1,128]{2,0,1:T(8,128)(2,1)}, u32[]{:S(2)}) copy-start(bf16[64,1,128]{2,0,1:T(8,128)(2,1)} %param.7) | copy-start | bytes 49156

commit v2 on v1

--- a/solution.py
+++ b/solution.py
@@ -10,6 +10,7 @@
 
 BLK = 128
 WIN = 512
+VMEM = 67043328
 LOG2E = 1.4426950408889634
 NT = (((1,), (1,)), ((), ()))
 
@@ -23,8 +24,8 @@
 
 
 def refresh_kernel(
-    n, start_ref, slot_ref, q_hbm, k_hbm, c_hbm, rel_ref, bank_ref,
-    q_v, q_t, keys, cache, mine, parts, bank,
+    n, start_hbm, slot_hbm, q_hbm, k_hbm, c_hbm, rel_ref, bank_ref,
+    start_ref, slot_ref, q_v, q_t, keys, cache, mine, parts, bank,
     load_sem, ks_sem, kr_sem, cs_sem, cr_sem, ps_sem, pr_sem,
 ):
     group, toks, dim = q_v.shape
@@ -40,19 +41,30 @@
     load_k = pltpu.make_async_copy(k_hbm, keys.at[me], load_sem.at[0])
     load_q = pltpu.make_async_copy(q_hbm, q_v, load_sem.at[1])
     load_c = pltpu.make_async_copy(c_hbm, cache.at[me], load_sem.at[2])
+    load_w = pltpu.make_async_copy(start_hbm, start_ref, load_sem.at[3])
+    load_s = pltpu.make_async_copy(slot_hbm, slot_ref, load_sem.at[4])
     load_k.start()
+    load_c.start()
     load_q.start()
-    load_c.start()
-
-    barrier = pltpu.get_barrier_semaphore()
-
-    def greet(i):
-        peer = lax.rem(me + 1 + i, n)
+    load_w.start()
+    load_s.start()
+
+    side = lax.rem(me, 2)
+    row = lax.div(me, 2)
+    height = n // 2
+    partner = me + 1 - 2 * side
+    above = row < height - 1
+    below = row > 0
+
+    def greet(peer):
         pl.semaphore_signal(
             barrier, inc=1, device_id={"seq": peer}, device_id_type=pl.DeviceIdType.MESH
         )
 
-    each(n - 1, greet)
+    barrier = pltpu.get_barrier_semaphore()
+    greet(partner)
+    pl.when(above)(lambda: greet(me + 2))
+    pl.when(below)(lambda: greet(me - 2))
 
     def link(src, dst, s_sem, r_sem, peer):
         return pltpu.make_async_remote_copy(
@@ -60,22 +72,38 @@
             device_id={"seq": peer}, device_id_type=pl.DeviceIdType.MESH,
         )
 
-    def key_copy(slot, peer):
-        return link(keys.at[slot], keys.at[slot], ks_sem.at[peer], kr_sem.at[slot], peer)
-
-    def cache_copy(slot, peer):
-        return link(cache.at[slot], cache.at[slot], cs_sem.at[peer], cr_sem.at[slot], peer)
+    def key_copy(slot, way, peer):
+        return link(keys.at[slot], keys.at[slot], ks_sem.at[way, slot], kr_sem.at[slot], peer)
+
+    def cache_copy(slot, way, peer):
+        return link(cache.at[slot], cache.at[slot], cs_sem.at[way, slot], cr_sem.at[slot], peer)
 
     def part_copy(slot, peer, src):
         return link(src, parts.at[slot], ps_sem.at[peer], pr_sem.at[slot], peer)
 
+    def chain(copy, act):
+        def column(slot, up, down):
+            if up:
+                pl.when(above)(lambda: act(copy(slot, 0, me + 2)))
+            if down:
+                pl.when(below)(lambda: act(copy(slot, 1, me - 2)))
+            act(copy(slot, 2, partner))
+        return column
+
+    send_key = chain(key_copy, lambda c: c.start())
+    send_cache = chain(cache_copy, lambda c: c.start())
+
     load_k.wait()
-    pl.semaphore_wait(barrier, n - 1)
-    each(n - 1, lambda i: key_copy(me, lax.rem(me + 1 + i, n)).start())
+    pl.semaphore_wait(
+        barrier, 1 + jnp.where(above, 1, 0) + jnp.where(below, 1, 0)
+    )
+    send_key(me, True, True)
     load_c.wait()
-    each(n - 1, lambda i: cache_copy(me, lax.rem(me + 1 + i, n)).start())
+    send_cache(me, True, True)
 
     load_q.wait()
+    load_w.wait()
+    load_s.wait()
     for j in range(group):
         q_t[:, j * toks:(j + 1) * toks] = q_v[j].T
 
@@ -102,15 +130,54 @@
 
     partial(me)
 
-    def arrive(i):
-        owner = lax.rem(me + n - 1 - i, n)
-        key_copy(owner, owner).wait_recv()
-        partial(owner)
-
-    each(n - 1, arrive)
+    def visit(s, copy, send):
+        def from_below():
+            copy(me - 2 * (s + 1), 0, me).wait_recv()
+            send(me - 2 * (s + 1), True, False)
+
+        def from_above():
+            copy(me + 2 * (s + 1), 1, me).wait_recv()
+            send(me + 2 * (s + 1), False, True)
+
+        pl.when(row - 1 - s >= 0)(from_below)
+        pl.when(row + 1 + s < height)(from_above)
+
+    def both(s, act, base):
+        pl.when(row - s >= 0)(lambda: act(base - 2 * s))
+        pl.when(row + s < height)(lambda: act(base + 2 * s))
+
+    def take_key(slot):
+        key_copy(slot, 2, me).wait_recv()
+        partial(slot)
+
+    def take_cache(slot):
+        cache_copy(slot, 2, me).wait_recv()
+
+    def key_step(s):
+        visit(s, key_copy, send_key)
+        if isinstance(s, int) and s == 0:
+            take_key(partner)
+        else:
+            both(s, take_key, partner)
+        both(s + 1, partial, me)
+        visit(s, cache_copy, send_cache)
+
+    key_step(0)
+    if height <= 4:
+        for s in range(1, height - 1):
+            key_step(s)
+    else:
+        lax.fori_loop(1, height - 1, lambda s, c: (key_step(s), c)[1], 0)
+    both(height - 1, take_key, partner)
+
     each(n - 1, lambda i: part_copy(me, lax.rem(me + 1 + i, n), mine).start())
 
-    each(n - 1, lambda i: cache_copy(lax.rem(me + n - 1 - i, n), me).wait_recv())
+    take_cache(partner)
+    if height <= 4:
+        for s in range(1, height):
+            both(s, take_cache, partner)
+    else:
+        lax.fori_loop(1, height, lambda s, c: (both(s, take_cache, partner), c)[1], 0)
     hits = jnp.where(
         lax.broadcasted_iota(jnp.int32, (slots, blocks), 0) == slot_ref[...], 1.0, 0.0
     )
@@ -138,12 +205,22 @@
     each(group, relate)
 
     def drain(i):
-        peer = lax.rem(me + 1 + i, n)
-        key_copy(me, peer).wait_send()
-        cache_copy(me, peer).wait_send()
-        part_copy(me, peer, mine).wait_send()
+        part_copy(me, lax.rem(me + 1 + i, n), mine).wait_send()
 
     each(n - 1, drain)
+    for copy in (key_copy, cache_copy):
+        done = chain(copy, lambda c: c.wait_send())
+        done(me, True, True)
+
+        def finish(s, done=done):
+            pl.when(row - s >= 0)(lambda: done(me - 2 * s, True, False))
+            pl.when(row + s < height)(lambda: done(me + 2 * s, False, True))
+
+        if height <= 4:
+            for s in range(1, height):
+                finish(s)
+        else:
+            lax.fori_loop(1, height, lambda s, c: (finish(s), c)[1], 0)
 
 
 def per_device(n, queries, new_keys, cache_keys, window_start, owner_slot):
@@ -151,7 +228,7 @@
     ktoks, local = new_keys.shape[0], cache_keys.shape[0]
     blocks = window_start.shape[0]
     slots = n * local
-    any_spec = pl.BlockSpec(memory_space=pl.ANY)
+    hbm_spec = pl.BlockSpec(memory_space=pltpu.HBM)
     vmem_spec = pl.BlockSpec(memory_space=pltpu.VMEM)
     bf16 = jnp.bfloat16
     rel, bank = pl.pallas_call(
@@ -160,11 +237,11 @@
             pltpu.VMEM((group, toks, slots), bf16),
             pltpu.VMEM((local, dim), bf16),
         ),
-        in_specs=[
-            pl.BlockSpec(memory_space=pltpu.SMEM), vmem_spec, any_spec, any_spec, any_spec,
-        ],
+        in_specs=[hbm_spec] * 5,
         out_specs=(vmem_spec, vmem_spec),
         scratch_shapes=[
+            pltpu.SMEM((blocks,), jnp.int32),
+            pltpu.VMEM((1, blocks), jnp.int32),
             pltpu.VMEM((group, toks, dim), bf16),
             pltpu.VMEM((dim, group * toks), bf16),
             pltpu.VMEM((n, ktoks, dim), bf16),
@@ -172,10 +249,11 @@
             pltpu.VMEM((blocks, dim), jnp.float32),
             pltpu.VMEM((n, blocks, dim), jnp.float32),
             pltpu.VMEM((slots, dim), bf16),
-            pltpu.SemaphoreType.DMA((3,)),
-        ] + [pltpu.SemaphoreType.DMA((n,))] * 6,
+            pltpu.SemaphoreType.DMA((5,)),
+        ] + [pltpu.SemaphoreType.DMA((3, n)), pltpu.SemaphoreType.DMA((n,))] * 2
+        + [pltpu.SemaphoreType.DMA((n,))] * 2,
         compiler_params=pltpu.CompilerParams(
-            collective_id=0, has_side_effects=True, vmem_limit_bytes=40 * 1024 * 1024
+            collective_id=0, has_side_effects=True, vmem_limit_bytes=VMEM - 2 * (group * toks * slots + local * dim) - 16384
         ),
         name="refresh",
     )(

time: 28.5 us -> 23.2 us (0.81)
  local copies, waits for them, and re-layouts: 4.6 us -> 1.53 us
  Pallas kernels: 22.9 us -> 20.9 us
    unnamed x12 -> x2, local copies, waits for them, and re-layouts: 4.6 us -> 1.53 us
    pallas_call x1, Pallas kernels: 22.9 us -> 20.9 us  [per_device(): pl.pallas_call(functools.partial(refresh_kernel, n), out_shape=(pltpu.VME...]
where the time goes in v2:
time: 23.2 us; the launch traced here: 23.1 us
  Pallas kernels  20.9 us (90%)
  local copies, waits for them, and re-layouts  1.53 us (7%)
  between operations  0.64 us (3%)
    pallas_call x1, Pallas kernels, per_device(): pl.pallas_call(functools.partial(refresh_kernel, n), out_shape=(pltpu.VME...  20.9 us
    unnamed x2, local copies, waits for them, and re-layouts  1.53 us

profile of v2, /device:TPU:0, one launch (start us, length us, event | category | flops | bytes accessed | tf_op | source)
XLA Modules:
  0.0 23.1 jit_solution(1018987542041050467)
XLA Ops:
  0.6 20.9 %refresh.1 = (bf16[7,128,512]{2,1,0:T(8,128)(2,1)S(1)}, bf16[64,128]{1,0:T(8,128)(2,1)S(1)}) custom-call(s32[8]{0:T(128)} %start_hbm.1, s32[1,8]{1,0:T(1,128)} %bitcast.11, bf16[7,128,128]{2,1,0:T(8,128)(2,1)} %bitcast.8, bf16[128,128]{1,0:T(8,128)(2,1)} %bitcast.9, bf16[64,128]{1,0:T(8,128)(2,1)} %bitcast.10), custom_call_target="tpu_custom_call" | custom-call | tf_op jit(solution)/shard_map/refresh/pallas_call | solution.py:234
  21.5 0.9 %copy.9 = bf16[128,7,512]{2,0,1:T(8,128)(2,1)} copy(bf16[128,7,512]{2,0,1:T(8,128)(2,1)S(1)} %bitcast.6) | data formatting | bytes 1835008
  22.4 0.6 %copy.10 = bf16[64,1,128]{2,0,1:T(8,128)(2,1)} copy(bf16[64,1,128]{2,0,1:T(8,128)(2,1)S(1)} %bitcast.7) | data formatting | bytes 32768

commit v3 on v1

--- a/solution.py
+++ b/solution.py
@@ -10,6 +10,7 @@
 
 BLK = 128
 WIN = 512
+VMEM = 67043328
 LOG2E = 1.4426950408889634
 NT = (((1,), (1,)), ((), ()))
 
@@ -23,8 +24,8 @@
 
 
 def refresh_kernel(
-    n, start_ref, slot_ref, q_hbm, k_hbm, c_hbm, rel_ref, bank_ref,
-    q_v, q_t, keys, cache, mine, parts, bank,
+    n, start_hbm, slot_hbm, q_hbm, k_hbm, c_hbm, q_v, bank,
+    start_ref, slot_ref, q_t, keys, cache, mine, parts,
     load_sem, ks_sem, kr_sem, cs_sem, cr_sem, ps_sem, pr_sem,
 ):
     group, toks, dim = q_v.shape
@@ -40,9 +41,13 @@
     load_k = pltpu.make_async_copy(k_hbm, keys.at[me], load_sem.at[0])
     load_q = pltpu.make_async_copy(q_hbm, q_v, load_sem.at[1])
     load_c = pltpu.make_async_copy(c_hbm, cache.at[me], load_sem.at[2])
+    load_w = pltpu.make_async_copy(start_hbm, start_ref, load_sem.at[3])
+    load_s = pltpu.make_async_copy(slot_hbm, slot_ref, load_sem.at[4])
     load_k.start()
+    load_c.start()
     load_q.start()
-    load_c.start()
+    load_w.start()
+    load_s.start()
 
     barrier = pltpu.get_barrier_semaphore()
 
@@ -73,9 +78,10 @@
     pl.semaphore_wait(barrier, n - 1)
     each(n - 1, lambda i: key_copy(me, lax.rem(me + 1 + i, n)).start())
     load_c.wait()
-    each(n - 1, lambda i: cache_copy(me, lax.rem(me + 1 + i, n)).start())
 
     load_q.wait()
+    load_w.wait()
+    load_s.wait()
     for j in range(group):
         q_t[:, j * toks:(j + 1) * toks] = q_v[j].T
 
@@ -109,6 +115,7 @@
 
     each(n - 1, arrive)
     each(n - 1, lambda i: part_copy(me, lax.rem(me + 1 + i, n), mine).start())
+    each(n - 1, lambda i: cache_copy(me, lax.rem(me + 1 + i, n)).start())
 
     each(n - 1, lambda i: cache_copy(lax.rem(me + n - 1 - i, n), me).wait_recv())
     hits = jnp.where(
@@ -129,14 +136,6 @@
     rep = (rep_sum * (1.0 / (group * WIN))).astype(jnp.bfloat16)
     placed = jnp.dot(hits, rep, preferred_element_type=jnp.float32)
     bank[...] = jnp.where(taken > 0.5, placed, old.astype(jnp.float32)).astype(jnp.bfloat16)
-    bank_ref[...] = bank[pl.ds(pl.multiple_of(me * local, local), local), :]
-
-    def relate(j):
-        r = lax.dot_general(q_v[j], bank[...], NT, preferred_element_type=jnp.float32)
-        rel_ref[j] = (r * scale).astype(jnp.bfloat16)
-
-    each(group, relate)
-
     def drain(i):
         peer = lax.rem(me + 1 + i, n)
         key_copy(me, peer).wait_send()
@@ -146,36 +145,53 @@
     each(n - 1, drain)
 
 
+def relate_kernel(q_v, bank, rel_hbm, bank_hbm, rel_v, sem):
+    group, toks, dim = q_v.shape
+    local = bank_hbm.shape[0]
+    scale = 1.0 / math.sqrt(dim)
+    first = pl.multiple_of(lax.axis_index("seq") * local, local)
+    keep = pltpu.make_async_copy(bank.at[pl.ds(first, local)], bank_hbm, sem.at[group])
+    keep.start()
+    outs = [
+        pltpu.make_async_copy(rel_v.at[j], rel_hbm.at[j], sem.at[j]) for j in range(group)
+    ]
+    for j in range(group):
+        r = lax.dot_general(q_v[j], bank[...], NT, preferred_element_type=jnp.float32)
+        rel_v[j] = (r * scale).astype(jnp.bfloat16)
+        outs[j].start()
+    for out in outs:
+        out.wait()
+    keep.wait()
+
+
 def per_device(n, queries, new_keys, cache_keys, window_start, owner_slot):
     toks, group, dim = queries.shape
     ktoks, local = new_keys.shape[0], cache_keys.shape[0]
     blocks = window_start.shape[0]
     slots = n * local
-    any_spec = pl.BlockSpec(memory_space=pl.ANY)
+    hbm_spec = pl.BlockSpec(memory_space=pltpu.HBM)
     vmem_spec = pl.BlockSpec(memory_space=pltpu.VMEM)
     bf16 = jnp.bfloat16
-    rel, bank = pl.pallas_call(
+    q_held, bank = pl.pallas_call(
         functools.partial(refresh_kernel, n),
         out_shape=(
-            pltpu.VMEM((group, toks, slots), bf16),
-            pltpu.VMEM((local, dim), bf16),
-        ),
-        in_specs=[
-            pl.BlockSpec(memory_space=pltpu.SMEM), vmem_spec, any_spec, any_spec, any_spec,
-        ],
+            pltpu.VMEM((group, toks, dim), bf16),
+            pltpu.VMEM((slots, dim), bf16),
+        ),
+        in_specs=[hbm_spec] * 5,
         out_specs=(vmem_spec, vmem_spec),
         scratch_shapes=[
-            pltpu.VMEM((group, toks, dim), bf16),
+            pltpu.SMEM((blocks,), jnp.int32),
+            pltpu.VMEM((1, blocks), jnp.int32),
             pltpu.VMEM((dim, group * toks), bf16),
             pltpu.VMEM((n, ktoks, dim), bf16),
             pltpu.VMEM((n, local, dim), bf16),
             pltpu.VMEM((blocks, dim), jnp.float32),
             pltpu.VMEM((n, blocks, dim), jnp.float32),
-            pltpu.VMEM((slots, dim), bf16),
-            pltpu.SemaphoreType.DMA((3,)),
+            pltpu.SemaphoreType.DMA((5,)),
         ] + [pltpu.SemaphoreType.DMA((n,))] * 6,
         compiler_params=pltpu.CompilerParams(
-            collective_id=0, has_side_effects=True, vmem_limit_bytes=40 * 1024 * 1024
+            collective_id=0, has_side_effects=True, vmem_limit_bytes=VMEM - 2 * dim * (group * toks + slots) - 16384
         ),
         name="refresh",
     )(
@@ -185,7 +201,24 @@
         new_keys.reshape(ktoks, dim),
         cache_keys.reshape(local, dim),
     )
-    return jnp.transpose(rel, (1, 0, 2)), bank[:, None, :]
+    rel, own = pl.pallas_call(
+        relate_kernel,
+        out_shape=(
+            jax.ShapeDtypeStruct((group, toks, slots), bf16),
+            jax.ShapeDtypeStruct((local, dim), bf16),
+        ),
+        in_specs=[vmem_spec, vmem_spec],
+        out_specs=(hbm_spec, hbm_spec),
+        scratch_shapes=[
+            pltpu.VMEM((group, toks, slots), bf16),
+            pltpu.SemaphoreType.DMA((group + 1,)),
+        ],
+        compiler_params=pltpu.CompilerParams(
+            vmem_limit_bytes=2 * group * toks * slots + 16 * 1024 * 1024
+        ),
+        name="relate",
+    )(q_held, bank)
+    return jnp.transpose(rel, (1, 0, 2)), own[:, None, :]
 
 
 def solution(mesh):

time: 28.5 us -> 22 us (0.77)
  local copies, waits for them, and re-layouts: 4.6 us -> 0 us
  Pallas kernels: 22.9 us -> 21.2 us
    unnamed x12 -> x0, local copies, waits for them, and re-layouts: 4.6 us -> none
    pallas_call x1, Pallas kernels: 22.9 us -> 20 us  [per_device(): pl.pallas_call(functools.partial(refresh_kernel, n), out_shape=(pltpu.VME...]
    pallas_call x0 -> x1, Pallas kernels: none -> 1.19 us  [per_device(): pl.pallas_call(relate_kernel, out_shape=(jax.ShapeDtypeStruct((group, tok...]
where the time goes in v3:
time: 22 us; the launch traced here: 21.8 us
  Pallas kernels  21.2 us (96%)
  between operations  0.64 us (3%)
    pallas_call x1, Pallas kernels, per_device(): pl.pallas_call(functools.partial(refresh_kernel, n), out_shape=(pltpu.VME...  20 us
    pallas_call x1, Pallas kernels, per_device(): pl.pallas_call(relate_kernel, out_shape=(jax.ShapeDtypeStruct((group, tok...  1.19 us

profile of v3, /device:TPU:0, one launch (start us, length us, event | category | flops | bytes accessed | tf_op | source)
XLA Modules:
  0.0 21.8 jit_solution(11399298456122732274)
XLA Ops:
  0.6 20.0 %refresh.1 = (bf16[7,128,128]{2,1,0:T(8,128)(2,1)S(1)}, bf16[512,128]{1,0:T(8,128)(2,1)S(1)}) custom-call(s32[8]{0:T(128)} %start_hbm.1, s32[1,8]{1,0:T(1,128)} %bitcast.9, bf16[7,128,128]{2,1,0:T(8,128)(2,1)} %bitcast.6, bf16[128,128]{1,0:T(8,128)(2,1)} %bitcast.7, bf16[64,128]{1,0:T(8,128)(2,1)} %bitcast.8), custom_call_target="tpu_custom_call" | custom-call | tf_op jit(solution)/shard_map/refresh/pallas_call | solution.py:175
  20.6 1.2 %relate.1 = (bf16[7,128,512]{2,1,0:T(8,128)(2,1)}, bf16[64,128]{1,0:T(8,128)(2,1)}) custom-call(bf16[7,128,128]{2,1,0:T(8,128)(2,1)S(1)} %get-tuple-element.6.q_v, bf16[512,128]{1,0:T(8,128)(2,1)S(1)} %get-tuple-element.7.bank), custom_call_target="tpu_custom_call" | custom-call | tf_op jit(solution)/shard_map/relate/pallas_call | solution.py:204

commit v4 on v3

--- a/solution.py
+++ b/solution.py
@@ -74,17 +74,13 @@
     def part_copy(slot, peer, src):
         return link(src, parts.at[slot], ps_sem.at[peer], pr_sem.at[slot], peer)
 
-    load_k.wait()
-    pl.semaphore_wait(barrier, n - 1)
-    each(n - 1, lambda i: key_copy(me, lax.rem(me + 1 + i, n)).start())
-    load_c.wait()
-
     load_q.wait()
     load_w.wait()
     load_s.wait()
     for j in range(group):
         q_t[:, j * toks:(j + 1) * toks] = q_v[j].T
 
+    load_k.wait()
     position = me * toks + lax.broadcasted_iota(jnp.int32, (1, toks), 1)
 
     def partial(owner):
@@ -108,6 +104,10 @@
 
     partial(me)
 
+    pl.semaphore_wait(barrier, n - 1)
+    each(n - 1, lambda i: key_copy(me, lax.rem(me + 1 + i, n)).start())
+    load_c.wait()
+
     def arrive(i):
         owner = lax.rem(me + n - 1 - i, n)
         key_copy(owner, owner).wait_recv()

time: 22 us -> 21.9 us (level)
  no operation moved by 1% of the time
where the time goes in v4:
time: 21.9 us; the launch traced here: 21.8 us
  Pallas kernels  21.2 us (97%)
  between operations  0.64 us (3%)
    pallas_call x1, Pallas kernels, per_device(): pl.pallas_call(functools.partial(refresh_kernel, n), out_shape=(pltpu.VME...  20 us
    pallas_call x1, Pallas kernels, per_device(): pl.pallas_call(relate_kernel, out_shape=(jax.ShapeDtypeStruct((group, tok...  1.19 us

profile of v4, /device:TPU:0, one launch (start us, length us, event | category | flops | bytes accessed | tf_op | source)
XLA Modules:
  0.0 21.8 jit_solution(12041000983757144145)
XLA Ops:
  0.6 20.0 %refresh.1 = (bf16[7,128,128]{2,1,0:T(8,128)(2,1)S(1)}, bf16[512,128]{1,0:T(8,128)(2,1)S(1)}) custom-call(s32[8]{0:T(128)} %start_hbm.1, s32[1,8]{1,0:T(1,128)} %bitcast.9, bf16[7,128,128]{2,1,0:T(8,128)(2,1)} %bitcast.6, bf16[128,128]{1,0:T(8,128)(2,1)} %bitcast.7, bf16[64,128]{1,0:T(8,128)(2,1)} %bitcast.8), custom_call_target="tpu_custom_call" | custom-call | tf_op jit(solution)/shard_map/refresh/pallas_call | solution.py:175
  20.6 1.2 %relate.1 = (bf16[7,128,512]{2,1,0:T(8,128)(2,1)}, bf16[64,128]{1,0:T(8,128)(2,1)}) custom-call(bf16[7,128,128]{2,1,0:T(8,128)(2,1)S(1)} %get-tuple-element.6.q_v, bf16[512,128]{1,0:T(8,128)(2,1)S(1)} %get-tuple-element.7.bank), custom_call_target="tpu_custom_call" | custom-call | tf_op jit(solution)/shard_map/relate/pallas_call | solution.py:204
